TPU v7x, 16 devices: a whole 2x2x2 slice. The times are simulated.
16 devices in a mesh: dp: 1, ep: 16 (over x, y, z, core).
Axes of the slice: x: 2, y: 2, z: 2, core: 2. Of those that a mesh axis runs over, the one named last changes fastest.
Arguments:
- x: bfloat16 [1, 16, 256, 2048], P('dp', 'ep')
- expert: int32 [1, 16, 256, 2], P('dp', 'ep')
- slot: int32 [1, 16, 256, 2], P('dp', 'ep')
- gate: float32 [1, 16, 256, 2], P('dp', 'ep')
- w_gate: bfloat16 [16, 2048, 14336], P('ep')
- w_up: bfloat16 [16, 2048, 14336], P('ep')
- w_down: bfloat16 [16, 14336, 2048], P('ep')
Outputs:
- y: bfloat16 [1, 16, 256, 2048], P('dp', 'ep')
All inputs are finite; a program needn't handle non-finite values.
Results may differ from a plain program's by a relative error of at most 0.009.
Values are sent between devices in bfloat16 or wider.
A program may use at most 2 GiB of HBM per device.

v0:
```python
import jax
import jax.numpy as jnp
from jax import lax
from jax.sharding import NamedSharding, PartitionSpec as P


def einsum(form, a, b):
    return jnp.einsum(form, a.astype(jnp.float32), b.astype(jnp.float32))


def solution(mesh):
    def placed(v, *spec):
        return lax.with_sharding_constraint(v, NamedSharding(mesh, P(*spec)))

    def step(x, expert, slot, gate, w_gate, w_up, w_down):
        experts, (tokens, top) = w_gate.shape[0], expert.shape[2:]
        slots = 5 * tokens * top // (4 * experts)
        to_expert = jax.nn.one_hot(expert, experts, dtype=jnp.bfloat16)
        to_slot = jax.nn.one_hot(slot, slots, dtype=jnp.bfloat16)
        weighted = to_expert * gate[..., None].astype(jnp.bfloat16)
        dispatch = einsum("abtke,abtkc->abtec", to_expert, to_slot).astype(jnp.bfloat16)
        combine = einsum("abtke,abtkc->abtec", weighted, to_slot).astype(jnp.bfloat16)
        z = einsum("abtec,abtd->aebcd", dispatch, x).astype(jnp.bfloat16)
        z = placed(z, "dp", None, "ep", None, None)
        z = placed(z, "dp", "ep", None, None, None)
        h = jax.nn.silu(einsum("aebcd,edf->aebcf", z, w_gate))
        h = (h * einsum("aebcd,edf->aebcf", z, w_up)).astype(jnp.bfloat16)
        out = einsum("aebcf,efd->aebcd", h, w_down).astype(jnp.bfloat16)
        out = placed(out, "dp", "ep", None, None, None)
        out = placed(out, "dp", None, "ep", None, None)
        y = einsum("abtec,aebcd->abtd", combine, out)
        return y.astype(jnp.bfloat16)

    return step
```

profile of v0, /device:TPU:0, one launch (start us, length us, event | category | flops | bytes accessed | tf_op | source)
XLA Modules:
  0.0 230.0 jit_solution(10995941109514443420)
XLA Ops:
  0.0 0.0 copy-start
  0.0 0.9 copy.3
  0.9 0.0 copy-start.3
  0.9 0.8 copy.5
  1.8 0.0 copy-done.3
  1.8 0.0 copy-start.5
  1.8 0.6 copy-done.5
  2.4 2.0 fusion.40
  4.4 0.8 copy.9
  5.3 0.0 copy-done
  5.3 0.9 fusion.23
  6.1 38.1 %all-to-all.4 = bf16[1,16,1,1,40,2048]{5,4,3,2,0,1:T(8,128)(2,1)S(1)} all-to-all(bf16[1,16,1,1,40,2048]{5,4,3,2,0,1:T(8,128)(2,1)S(1)} %fusion.23), channel_id=1, replica_groups=mesh['dp'=1,'ep'=16] {'ep'}, dimensions={1} | all-to-all | bytes 5242880 | tf_op jit(solution)/sharding_constraint;jit(solution)/sharding_constraint | solution.py:13
  44.3 0.0 copy-start.2
  44.3 1.5 copy-done.2
  45.7 45.1 %fusion.4 = f32[16,40,14336]{2,1,0:T(8,128)} fusion(bf16[1,2048,14336]{2,1,0:T(8,128)(2,1)} %param.4, bf16[1,16,1,1,40,2048]{5,4,3,2,0,1:T(8,128)(2,1)S(1)} %all-to-all.4), kind=kOutput, calls=%fused_computation.4 | convolution fusion | flops 37580963840 | bytes 98041856 | tf_op jit(solution)/aebcd,edf->aebcf/dot_general | solution.py:8
  90.8 51.4 %fusion.12.clone.8 = bf16[16,40,14336]{2,1,0:T(8,128)(2,1)} fusion(bf16[1,2048,14336]{2,1,0:T(8,128)(2,1)} %param.5, f32[16,40,14336]{2,1,0:T(8,128)} %fusion.4, bf16[1,16,1,1,40,2048]{5,4,3,2,0,1:T(8,128)(2,1)} %copy-done.2), kind=kOutput, calls=%fused_computation.13.clone.clone.clone.clone.clone.clone.clone.1 | convolution fusion | flops 37636014080 | bytes 116391936 | tf_op jit(solution)/aebcd,edf->aebcf/dot_general | solution.py:8
  142.3 0.0 copy-start.7
  142.3 0.0 copy-start.4
  142.3 0.0 copy-start.6
  142.3 0.0 copy-start.1
  142.3 45.6 %fusion.24 = bf16[1,1,16,1,40,2048]{5,4,3,1,0,2:T(8,128)(2,1)} fusion(bf16[1,14336,2048]{2,1,0:T(8,128)(2,1)} %param.6, bf16[16,40,14336]{2,1,0:T(8,128)(2,1)} %fusion.12.clone.8), kind=kOutput, calls=%fused_computation.18 | convolution fusion | flops 37582274560 | bytes 79691776 | tf_op jit(solution)/aebcf,efd->aebcd/dot_general | solution.py:8
  187.9 3.2 %all-to-all-start.1 = ((bf16[1,1,16,1,40,2048]{5,4,3,1,0,2:T(8,128)(2,1)}), bf16[1,1,16,1,40,2048]{5,4,3,1,0,2:T(8,128)(2,1)}, u32[]{:S(2)}, u32[]{:S(2)}) async-start(bf16[1,1,16,1,40,2048]{5,4,3,1,0,2:T(8,128)(2,1)} %fusion.24), calls=%async_computation.1 | async-start | bytes 5242880 | tf_op jit(solution)/sharding_constraint;jit(solution)/sharding_constraint | solution.py:13
  191.1 0.0 copy-done.7
  191.1 0.1 copy.4
  191.2 0.0 copy-done.4
  191.2 0.0 copy-done.6
  191.2 2.4 %fusion.43 = bf16[256,16,40]{2,1,0:T(8,128)(2,1)S(1)} fusion(s32[256,2]{1,0:T(8,128)S(1)} %copy-done.6, s32[256,2]{1,0:T(8,128)S(1)} %copy-done.4, bf16[256,2]{1,0:T(8,128)(2,1)S(1)} %copy.4), kind=kOutput, calls=%fused_computation.29 | convolution fusion | flops 692224 | bytes 332800 | tf_op jit(solution)/abtke,abtkc->abtec/dot_general | solution.py:8
  193.7 0.8 copy.8
  194.5 31.7 %all-to-all-done.1 = bf16[1,1,16,1,40,2048]{5,4,3,1,0,2:T(8,128)(2,1)} async-done(((bf16[1,1,16,1,40,2048]{5,4,3,1,0,2:T(8,128)(2,1)}), bf16[1,1,16,1,40,2048]{5,4,3,1,0,2:T(8,128)(2,1)}, u32[]{:S(2)}, u32[]{:S(2)}) %all-to-all-start.1) | async-done | bytes 2621472 | tf_op jit(solution)/sharding_constraint;jit(solution)/sharding_constraint | solution.py:13
  226.2 3.7 %fusion.36 = bf16[1,1,256,2048]{3,2,1,0:T(8,128)(2,1)} fusion(bf16[1,1,16,1,40,2048]{5,4,3,1,0,2:T(8,128)(2,1)} %all-to-all-done.1, bf16[256,16,40]{0,2,1:T(8,128)(2,1)S(1)} %copy.8), kind=kOutput, calls=%fused_computation.24 | convolution fusion | flops 671612928 | bytes 3997696 | tf_op jit(solution)/abtec,aebcd->abtd/dot_general | solution.py:8
  230.0 0.0 copy-done.1
  (1 shorter events, 0.0 us)
Async XLA Ops:
  0.0 5.3 %copy-start = (bf16[1,1,256,2048]{3,2,1,0:T(8,128)(2,1)S(1)}, bf16[1,1,256,2048]{3,2,1,0:T(8,128)(2,1)}, u32[]{:S(2)}) copy-start(bf16[1,1,256,2048]{3,2,1,0:T(8,128)(2,1)} %param.3) | copy-start | bytes 3145732
  0.9 0.9 copy-start.3
  1.8 0.7 copy-start.5
  44.3 1.5 copy-start.2
  142.3 48.8 %copy-start.7 = (f32[1,1,256,2]{2,3,1,0:T(2,128)S(1)}, f32[1,1,256,2]{2,3,1,0:T(2,128)}, u32[]{:S(2)}) copy-start(f32[1,1,256,2]{2,3,1,0:T(2,128)} %param.1) | copy-start | bytes 6148
  142.3 49.0 %copy-start.4 = (s32[256,2]{1,0:T(8,128)S(1)}, s32[256,2]{1,0:T(8,128)}, u32[]{:S(2)}) copy-start(s32[256,2]{1,0:T(8,128)} %copy-done.3) | copy-start | bytes 6148
  142.3 49.0 %copy-start.6 = (s32[256,2]{1,0:T(8,128)S(1)}, s32[256,2]{1,0:T(8,128)}, u32[]{:S(2)}) copy-start(s32[256,2]{1,0:T(8,128)} %copy-done.5) | copy-start | bytes 6148
  142.3 87.7 %copy-start.1 = (bf16[1,1,256,2048]{3,2,1,0:T(8,128)(2,1)S(1)}, bf16[1,1,256,2048]{3,2,1,0:T(8,128)(2,1)}, u32[]{:S(2)}) copy-start(bf16[1,1,256,2048]{3,2,1,0:T(8,128)(2,1)} %param.3) | copy-start | bytes 3145732
  187.9 38.4 %all-to-all-start.1 = ((bf16[1,1,16,1,40,2048]{5,4,3,1,0,2:T(8,128)(2,1)}), bf16[1,1,16,1,40,2048]{5,4,3,1,0,2:T(8,128)(2,1)}, u32[]{:S(2)}, u32[]{:S(2)}) async-start(bf16[1,1,16,1,40,2048]{5,4,3,1,0,2:T(8,128)(2,1)} %fusion.24), calls=%async_computation.1 | async-start | bytes 5242880 | tf_op jit(solution)/sharding_constraint;jit(solution)/sharding_constraint | solution.py:13
where the time goes:
time: 230 us
  matrix products  151 us (66%)
  blocking collectives  38.1 us (17%)
  waiting for transfers between devices  31.7 us (14%)
  local copies, waits for them, and re-layouts  5.71 us (2%)
  starting transfers between devices  3.19 us (1%)
    dot_general x7, matrix products, einsum(): return jnp.einsum(form, a.astype(jnp.float32), b.astype(jnp.float32))  151 us
    another operation x1, blocking collectives, placed(): return lax.with_sharding_constraint(v, NamedSharding(mesh, P(*spec)))  38.1 us
    another operation x1, waiting for transfers between devices, placed(): return lax.with_sharding_constraint(v, NamedSharding(mesh, P(*spec)))  31.7 us
  transfers between devices with their start and end apart: 1, of which 1 were waited for; matrix products, arithmetic and copies ran while one was open for 1% of the time, Pallas kernels for 0%

commit v1 on v0

v1 whole, which is shorter than its diff:
```python
import functools

import jax
import jax.numpy as jnp
from jax import lax
from jax.experimental import pallas as pl
from jax.experimental.pallas import tpu as pltpu
from jax.sharding import PartitionSpec as P

MESH = pl.DeviceIdType.MESH
ORDER = (0, 1, 2, 4, 8, 3, 5, 9, 6, 10, 12, 7, 11, 13, 14, 15)
SENDS = ORDER[1:]
FAR_FIRST = tuple(reversed(SENDS))
NEAR = 8
FT = 512
NT = 256
BUFS = 3
COMM = True


def partner(me, mask):
    out = me
    for b in range(4):
        if mask >> b & 1:
            out = out + (1 << b) * (1 - 2 * ((me // (1 << b)) % 2))
    return out


def kernel(dims, x_hbm, expert_hbm, slot_hbm, gate_hbm, wg_hbm, wu_hbm, wd_hbm, y_ref,
           x, expert, slot, gate, z_send, z_recv, z, weight, h, wg, wu, wd, o_send, o_recv,
           in_sem, w_sem, d_sem, zs_sem, zr_sem, os_sem, or_sem):
    n, slots, tokens, d, ff = dims
    rows, near = n * slots, NEAR * slots
    f_tiles, n_tiles = ff // FT, d // NT
    me = lax.axis_index("ep")
    f32, bf16 = jnp.float32, jnp.bfloat16

    def device(mask):
        return {"ep": partner(me, mask)}

    ins = [pltpu.make_async_copy(a, b, in_sem.at[i]) for i, (a, b) in enumerate(
        ((x_hbm, x), (expert_hbm, expert), (slot_hbm, slot), (gate_hbm, gate)))]
    for c in ins:
        c.start()

    def fetch(i):
        columns = pl.ds(pl.multiple_of((i % f_tiles) * FT, FT), FT)
        s = i % BUFS
        return (pltpu.make_async_copy(wg_hbm.at[:, columns], wg.at[s], w_sem.at[0, s]),
                pltpu.make_async_copy(wu_hbm.at[:, columns], wu.at[s], w_sem.at[1, s]))

    def fetch_down(i):
        columns = pl.ds(pl.multiple_of(i * NT, NT), NT)
        return pltpu.make_async_copy(wd_hbm.at[:, columns], wd.at[i % 2], d_sem.at[i % 2])

    if COMM:
        barrier = pltpu.get_barrier_semaphore()
        for mask in SENDS:
            pl.semaphore_signal(barrier, inc=1, device_id=device(mask), device_id_type=MESH)

    for i in range(BUFS - 1):
        for c in fetch(i):
            c.start()

    for c in ins:
        c.wait()
    place = jnp.where(slot[...] < slots, (expert[...] ^ me) * slots + slot[...], -1)
    at = lax.broadcasted_iota(jnp.int32, (rows, tokens), 0)
    first, second = at == place[0:1, :], at == place[1:2, :]
    pick = jnp.where(first | second, 1.0, 0.0).astype(bf16)
    g = gate[...].astype(bf16).astype(f32)
    zero = jnp.zeros((rows, tokens), f32)
    weight[...] = (jnp.where(first, g[0:1, :], zero) + jnp.where(second, g[1:2, :], zero)).T.astype(bf16)
    sent = jnp.dot(pick, x[...], preferred_element_type=f32)
    for m in range(n):
        (z_recv if m == 0 else z_send)[m] = sent[m * slots:(m + 1) * slots].astype(bf16)

    def send_z(mask):
        return pltpu.make_async_remote_copy(
            src_ref=z_send.at[mask], dst_ref=z_recv.at[mask], send_sem=zs_sem.at[mask], recv_sem=zr_sem.at[mask],
            device_id=device(mask), device_id_type=MESH)

    if COMM:
        pl.semaphore_wait(barrier, n - 1)
        for mask in SENDS:
            send_z(mask).start()

    def settle(lo, hi):
        if COMM:
            for p in range(lo, hi):
                if ORDER[p]:
                    send_z(ORDER[p]).wait_recv()
        for p in range(lo, hi, 2):
            pair = [z_recv[ORDER[q]].astype(f32) for q in (p, p + 1)]
            z[p * slots:(p + 2) * slots, :] = jnp.concatenate(pair, axis=0).astype(bf16)

    def up(first_tile, last_tile, row, count):
        @pl.loop(first_tile, last_tile)
        def _(i):
            s = i % BUFS
            for c in fetch(i):
                c.wait()

            @pl.when(i + BUFS - 1 < 2 * f_tiles)
            def _():
                for c in fetch(i + BUFS - 1):
                    c.start()

            @pl.when(i == 2 * f_tiles - BUFS)
            def _():
                fetch_down(0).start()

            zz = z[row:row + count, :]
            a = jnp.dot(zz, wg[s], preferred_element_type=f32)
            b = jnp.dot(zz, wu[s], preferred_element_type=f32)
            columns = pl.ds(pl.multiple_of((i % f_tiles) * FT, FT), FT)
            h[row:row + count, columns] = (a * jax.nn.sigmoid(a) * b).astype(bf16)

    settle(0, NEAR)
    up(0, f_tiles, 0, near)
    settle(NEAR, n)
    up(f_tiles, 2 * f_tiles, near, rows - near)

    def send_o(t, mask):
        return pltpu.make_async_remote_copy(
            src_ref=o_send.at[t, mask], dst_ref=o_recv.at[t, mask], send_sem=os_sem.at[t], recv_sem=or_sem.at[t],
            device_id=device(mask), device_id_type=MESH)

    def combine(t):
        if COMM:
            arrived = o_recv.at[t, pl.ds(1, n - 1)]
            pltpu.make_async_copy(arrived, arrived, or_sem.at[t]).wait()
        back = jnp.concatenate([o_recv[t, m].astype(f32) for m in range(n)], axis=0).astype(bf16)
        y_ref[:, pl.ds(pl.multiple_of(t * NT, NT), NT)] = jnp.dot(
            weight[...], back, preferred_element_type=f32).astype(bf16)

    @pl.loop(0, n_tiles)
    def _(t):
        fetch_down(t).wait()

        @pl.when(t + 1 < n_tiles)
        def _():
            fetch_down(t + 1).start()

        o = jnp.dot(h[...], wd[t % 2], preferred_element_type=f32)
        for p in range(n):
            m = ORDER[p]
            (o_send if m else o_recv)[t, m] = o[p * slots:(p + 1) * slots].astype(bf16)
        if COMM:
            for mask in FAR_FIRST:
                send_o(t, mask).start()

        @pl.when(t >= 2)
        def _():
            combine(t - 2)

    for t in range(n_tiles - 2, n_tiles):
        combine(t)
    if COMM:
        for mask in SENDS:
            send_z(mask).wait_send()
        for t in range(n_tiles):
            left = o_send.at[t, pl.ds(1, n - 1)]
            pltpu.make_async_copy(left, left, os_sem.at[t]).wait()


def solution(mesh):
    n = mesh.shape["ep"]

    def local(x, expert, slot, gate, w_gate, w_up, w_down):
        _, d, ff = w_gate.shape
        tokens, top = expert.shape[2:]
        slots = 5 * tokens * top // (4 * n)
        rows = n * slots
        n_tiles = d // NT
        bf16 = jnp.bfloat16
        any_ = pl.BlockSpec(memory_space=pl.ANY)
        y = pl.pallas_call(
            functools.partial(kernel, (n, slots, tokens, d, ff)),
            out_shape=jax.ShapeDtypeStruct((tokens, d), bf16),
            in_specs=[any_] * 7,
            out_specs=pl.BlockSpec(memory_space=pltpu.VMEM),
            scratch_shapes=[
                pltpu.VMEM((tokens, d), bf16),
                pltpu.VMEM((top, tokens), jnp.int32),
                pltpu.VMEM((top, tokens), jnp.int32),
                pltpu.VMEM((top, tokens), jnp.float32),
                pltpu.VMEM((n, slots, d), bf16),
                pltpu.VMEM((n, slots, d), bf16),
                pltpu.VMEM((rows, d), bf16),
                pltpu.VMEM((tokens, rows), bf16),
                pltpu.VMEM((rows, ff), bf16),
                pltpu.VMEM((BUFS, d, FT), bf16),
                pltpu.VMEM((BUFS, d, FT), bf16),
                pltpu.VMEM((2, ff, NT), bf16),
                pltpu.VMEM((n_tiles, n, slots, NT), bf16),
                pltpu.VMEM((n_tiles, n, slots, NT), bf16),
                pltpu.SemaphoreType.DMA((4,)),
                pltpu.SemaphoreType.DMA((2, BUFS)),
                pltpu.SemaphoreType.DMA((2,)),
                pltpu.SemaphoreType.DMA((n,)),
                pltpu.SemaphoreType.DMA((n,)),
                pltpu.SemaphoreType.DMA((n_tiles,)),
                pltpu.SemaphoreType.DMA((n_tiles,)),
            ],
            compiler_params=pltpu.CompilerParams(
                vmem_limit_bytes=67043328,
                **(dict(collective_id=0, has_side_effects=True) if COMM else {})),
        )(x[0, 0], expert[0, 0].T, slot[0, 0].T, gate[0, 0].T, w_gate[0], w_up[0], w_down[0])
        return y[None, None]

    tok, exp = P("dp", "ep", None, None), P("ep", None, None)
    return jax.shard_map(local, mesh=mesh, in_specs=(tok,) * 4 + (exp,) * 3, out_specs=tok, check_vma=False)
```

time: 230 us -> 157 us (0.68)
  Pallas kernels: 0 us -> 155 us
  matrix products: 151 us -> 0 us
  blocking collectives: 38.1 us -> 0 us
  waiting for transfers between devices: 31.7 us -> 0 us
  local copies, waits for them, and re-layouts: 5.71 us -> 2.3 us
  starting transfers between devices: 3.19 us -> 0 us
    pallas_call x0 -> x1, Pallas kernels: none -> 155 us  [local(): pl.pallas_call(functools.partial(kernel, (n, slots, tokens, d, ff)), out_...]
    dot_general x7 -> x0, matrix products: 151 us -> none  [einsum(): return jnp.einsum(form, a.astype(jnp.float32), b.astype(jnp.float32))]
    another operation x1 -> x0, blocking collectives: 38.1 us -> none  [placed(): return lax.with_sharding_constraint(v, NamedSharding(mesh, P(*spec)))]
    another operation x1 -> x0, waiting for transfers between devices: 31.7 us -> none  [placed(): return lax.with_sharding_constraint(v, NamedSharding(mesh, P(*spec)))]
    another operation x1 -> x0, starting transfers between devices: 3.19 us -> none  [placed(): return lax.with_sharding_constraint(v, NamedSharding(mesh, P(*spec)))]
  transfers between devices with their start and end apart: 1 -> 0, of which waited for: 1 -> 0; matrix products, arithmetic and copies ran while one was open for 1% -> 0% of each run, Pallas kernels for 0% -> 0%
where the time goes in v1:
time: 157 us
  Pallas kernels  155 us (99%)
  local copies, waits for them, and re-layouts  2.3 us (1%)
    pallas_call x1, Pallas kernels, local(): pl.pallas_call(functools.partial(kernel, (n, slots, tokens, d, ff)), out_...  155 us

profile of v1, /device:TPU:0, one launch (start us, length us, event | category | flops | bytes accessed | tf_op | source)
XLA Modules:
  0.0 157.0 jit_solution(12136736806999186414)
XLA Ops:
  0.0 154.7 %shard_map.73 = bf16[256,2048]{1,0:T(8,128)(2,1)} custom-call(bf16[256,2048]{1,0:T(8,128)(2,1)} %bitcast.18, s32[2,256]{1,0:T(2,128)} %bitcast.19, s32[2,256]{1,0:T(2,128)} %bitcast.20, f32[2,256]{1,0:T(2,128)} %bitcast.21, bf16[2048,14336]{1,0:T(8,128)(2,1)} %bitcast.14, bf16[2048,14336]{1,0:T(8,128)(2,1)} %bitcast.15, bf16[14336,2048]{1,0:T(8,128)(2,1)} %bitcast.16), custom_call_target="tpu_custom_call" | custom-call | tf_op jit(solution)/shard_map/pallas_call | solution.py:178
  154.7 2.3 %copy.9 = bf16[1,1,256,2048]{3,2,1,0:T(8,128)(2,1)} copy(bf16[1,1,256,2048]{3,2,1,0:T(8,128)(2,1)} %bitcast.17) | data formatting | bytes 2097152

commit v2 on v1

v2 whole, which is shorter than its diff:
```python
import functools

import jax
import jax.numpy as jnp
from jax import lax
from jax.experimental import pallas as pl
from jax.experimental.pallas import tpu as pltpu
from jax.sharding import PartitionSpec as P

MESH = pl.DeviceIdType.MESH
ORDER = (0, 1, 2, 4, 8, 3, 5, 9, 6, 10, 12, 7, 11, 13, 14, 15)
SENDS = ORDER[1:]
FAR_FIRST = tuple(reversed(SENDS))
NEAR = 8
FT = 512
NT = 256
PAIR = 2
RING = 3
EARLY = 8
LAG = 5
COMM = True


def partner(me, mask):
    out = me
    for b in range(4):
        if mask >> b & 1:
            out = out + (1 << b) * (1 - 2 * ((me // (1 << b)) % 2))
    return out


def kernel(dims, x_hbm, expert_hbm, slot_hbm, gate_hbm, wg_hbm, wu_hbm, wd_hbm, y_ref,
           x, expert, slot, gate, z_send, z_recv, z, weight, h, pool, o_send, o_recv,
           in_sem, w_sem, d_sem, zs_sem, zr_sem, os_sem, or_sem):
    n, slots, tokens, d, ff = dims
    rows, near = n * slots, NEAR * slots
    groups, n_tiles, chunks = ff // (FT * PAIR), d // NT, ff // d
    steps = groups + EARLY
    turn = (RING - steps) % RING
    me = lax.axis_index("ep")
    f32, bf16 = jnp.float32, jnp.bfloat16

    def device(mask):
        return {"ep": partner(me, mask)}

    if COMM:
        barrier = pltpu.get_barrier_semaphore()
        for mask in SENDS:
            pl.semaphore_signal(barrier, inc=1, device_id=device(mask), device_id_type=MESH)

    ins = [pltpu.make_async_copy(a, b, in_sem.at[i]) for i, (a, b) in enumerate(
        ((x_hbm, x), (expert_hbm, expert), (slot_hbm, slot), (gate_hbm, gate)))]
    for c in ins:
        c.start()

    def place_of(q, u):
        column = ((q % groups) * PAIR + u) * FT
        return 2 * (PAIR * ((q + turn) % RING) + u), pl.ds(pl.multiple_of(column, FT), FT)

    def fetch(q):
        copies = []
        for u in range(PAIR):
            s, columns = place_of(q, u)
            copies.append(pltpu.make_async_copy(wg_hbm.at[:, columns], pool.at[s], w_sem.at[s]))
            copies.append(pltpu.make_async_copy(wu_hbm.at[:, columns], pool.at[s + 1], w_sem.at[s + 1]))
        return copies

    def half(t):
        return pl.ds(pl.multiple_of((t % 2) * NT, NT), NT)

    def fetch_down(t, ks=None):
        columns = pl.ds(pl.multiple_of(t * NT, NT), NT)
        return [pltpu.make_async_copy(wd_hbm.at[pl.ds(k * d, d), columns], pool.at[k, :, half(t)], d_sem.at[t % 2, k])
                for k in (range(chunks) if ks is None else ks)]

    for c in fetch(0):
        c.start()

    for c in ins:
        c.wait()
    place = jnp.where(slot[...] < slots, (expert[...] ^ me) * slots + slot[...], -1)
    at = lax.broadcasted_iota(jnp.int32, (rows, tokens), 0)
    first, second = at == place[0:1, :], at == place[1:2, :]
    pick = jnp.where(first | second, 1.0, 0.0).astype(bf16)
    g = gate[...].astype(bf16).astype(f32)
    zero = jnp.zeros((rows, tokens), f32)
    weight[...] = (jnp.where(first, g[0:1, :], zero) + jnp.where(second, g[1:2, :], zero)).T.astype(bf16)
    sent = jnp.dot(pick, x[...], preferred_element_type=f32)
    for m in range(n):
        (z_recv if m == 0 else z_send)[m] = sent[m * slots:(m + 1) * slots].astype(bf16)

    def send_z(mask):
        return pltpu.make_async_remote_copy(
            src_ref=z_send.at[mask], dst_ref=z_recv.at[mask], send_sem=zs_sem.at[mask], recv_sem=zr_sem.at[mask],
            device_id=device(mask), device_id_type=MESH)

    if COMM:
        pl.semaphore_wait(barrier, n - 1)
        for mask in SENDS:
            send_z(mask).start()
    for q in range(1, RING):
        for c in fetch(q):
            c.start()

    def settle(lo, hi):
        if COMM:
            for p in range(lo, hi):
                if ORDER[p]:
                    send_z(ORDER[p]).wait_recv()
        for p in range(lo, hi, 2):
            pair = [z_recv[ORDER[q]].astype(f32) for q in (p, p + 1)]
            z[p * slots:(p + 2) * slots, :] = jnp.concatenate(pair, axis=0).astype(bf16)

    def up(q, row, count):
        rows_ = z[row:row + count, :]
        for u in range(PAIR):
            s, columns = place_of(q, u)
            a = jnp.dot(rows_, pool[s], preferred_element_type=f32)
            b = jnp.dot(rows_, pool[s + 1], preferred_element_type=f32)
            h[row:row + count, columns] = (a * jax.nn.sigmoid(a) * b).astype(bf16)

    def ready(q):
        for c in fetch(q):
            c.wait()

    def refill(q):
        @pl.when(q + RING - 1 < steps)
        def _():
            for c in fetch(q + RING - 1):
                c.start()

    settle(0, 4)

    @pl.loop(0, RING)
    def _(q):
        ready(q)
        up(q, 0, near // 2)

    settle(4, NEAR)

    @pl.loop(0, RING)
    def _(q):
        @pl.when(q > 0)
        def _():
            refill(q)

        up(q, near // 2, near // 2)

    @pl.loop(RING, EARLY)
    def _(q):
        ready(q)
        refill(q)
        up(q, 0, near)

    settle(NEAR, n)

    @pl.loop(EARLY, groups)
    def _(q):
        ready(q)
        refill(q)
        up(q, 0, rows)

    split = 2 * PAIR

    @pl.loop(groups, steps)
    def _(q):
        ready(q)
        refill(q)

        @pl.when(q == steps - 2)
        def _():
            for c in fetch_down(0, range(split)):
                c.start()

        @pl.when(q == steps - 1)
        def _():
            for c in fetch_down(0, range(split, chunks)) + fetch_down(1):
                c.start()

        up(q, near, rows - near)

    def send_o(t, mask):
        return pltpu.make_async_remote_copy(
            src_ref=o_send.at[t, mask], dst_ref=o_recv.at[t, mask], send_sem=os_sem.at[t], recv_sem=or_sem.at[t],
            device_id=device(mask), device_id_type=MESH)

    def combine(t):
        for u in (t, t + 1):
            if COMM:
                arrived = o_recv.at[u, pl.ds(1, n - 1)]
                pltpu.make_async_copy(arrived, arrived, or_sem.at[u]).wait()
        for u in (t, t + 1):
            back = jnp.concatenate([o_recv[u, m].astype(f32) for m in range(n)], axis=0).astype(bf16)
            y_ref[:, pl.ds(pl.multiple_of(u * NT, NT), NT)] = jnp.dot(
                weight[...], back, preferred_element_type=f32).astype(bf16)

    @pl.loop(0, n_tiles)
    def _(t):
        for c in fetch_down(t):
            c.wait()

        @pl.when((t >= 1) & (t + 1 < n_tiles))
        def _():
            for c in fetch_down(t + 1):
                c.start()

        w = pool[0:chunks, :, half(t)].reshape(ff, NT)
        o = jnp.dot(h[...], w, preferred_element_type=f32)
        for p in range(n):
            m = ORDER[p]
            (o_send if m else o_recv)[t, m] = o[p * slots:(p + 1) * slots].astype(bf16)
        if COMM:
            for mask in FAR_FIRST:
                send_o(t, mask).start()

        @pl.when((t >= LAG) & (t % 2 == LAG % 2))
        def _():
            combine(t - LAG)

    for t in range((n_tiles - LAG + 1) // 2 * 2, n_tiles, 2):
        combine(t)
    if COMM:
        for mask in SENDS:
            send_z(mask).wait_send()
        for t in range(n_tiles):
            left = o_send.at[t, pl.ds(1, n - 1)]
            pltpu.make_async_copy(left, left, os_sem.at[t]).wait()


def solution(mesh):
    n = mesh.shape["ep"]

    def local(x, expert, slot, gate, w_gate, w_up, w_down):
        _, d, ff = w_gate.shape
        tokens, top = expert.shape[2:]
        slots = 5 * tokens * top // (4 * n)
        rows = n * slots
        n_tiles = d // NT
        bf16 = jnp.bfloat16
        any_ = pl.BlockSpec(memory_space=pl.ANY)
        y = pl.pallas_call(
            functools.partial(kernel, (n, slots, tokens, d, ff)),
            out_shape=pltpu.VMEM((tokens, d), bf16),
            in_specs=[any_] * 7,
            out_specs=pl.BlockSpec(memory_space=pltpu.VMEM),
            scratch_shapes=[
                pltpu.VMEM((tokens, d), bf16),
                pltpu.VMEM((top, tokens), jnp.int32),
                pltpu.VMEM((top, tokens), jnp.int32),
                pltpu.VMEM((top, tokens), jnp.float32),
                pltpu.VMEM((n, slots, d), bf16),
                pltpu.VMEM((n, slots, d), bf16),
                pltpu.VMEM((rows, d), bf16),
                pltpu.VMEM((tokens, rows), bf16),
                pltpu.VMEM((rows, ff), bf16),
                pltpu.VMEM((2 * PAIR * RING, d, FT), bf16),
                pltpu.VMEM((n_tiles, n, slots, NT), bf16),
                pltpu.VMEM((n_tiles, n, slots, NT), bf16),
                pltpu.SemaphoreType.DMA((4,)),
                pltpu.SemaphoreType.DMA((2 * PAIR * RING,)),
                pltpu.SemaphoreType.DMA((2, ff // d)),
                pltpu.SemaphoreType.DMA((n,)),
                pltpu.SemaphoreType.DMA((n,)),
                pltpu.SemaphoreType.DMA((n_tiles,)),
                pltpu.SemaphoreType.DMA((n_tiles,)),
            ],
            compiler_params=pltpu.CompilerParams(
                vmem_limit_bytes=67043328 - 2 * tokens * d - (1 << 16),
                **(dict(collective_id=0, has_side_effects=True) if COMM else {})),
        )(x[0, 0], expert[0, 0].T, slot[0, 0].T, gate[0, 0].T, w_gate[0], w_up[0], w_down[0])
        return y[None, None]

    tok, exp = P("dp", "ep", None, None), P("ep", None, None)
    return jax.shard_map(local, mesh=mesh, in_specs=(tok,) * 4 + (exp,) * 3, out_specs=tok, check_vma=False)
```

time: 157 us -> 147 us (0.936)
  Pallas kernels: 155 us -> 146 us
    pallas_call x1, Pallas kernels: 155 us -> 146 us  [local(): pl.pallas_call(functools.partial(kernel, (n, slots, tokens, d, ff)), out_...]
where the time goes in v2:
time: 147 us
  Pallas kernels  146 us (99%)
    pallas_call x1, Pallas kernels, local(): pl.pallas_call(functools.partial(kernel, (n, slots, tokens, d, ff)), out_...  146 us

profile of v2, /device:TPU:0, one launch (start us, length us, event | category | flops | bytes accessed | tf_op | source)
XLA Modules:
  0.0 147.0 jit_solution(18221632415288797320)
XLA Ops:
  0.0 146.0 %shard_map.73 = bf16[256,2048]{1,0:T(8,128)(2,1)S(1)} custom-call(bf16[256,2048]{1,0:T(8,128)(2,1)} %bitcast.18, s32[2,256]{1,0:T(2,128)} %bitcast.19, s32[2,256]{1,0:T(2,128)} %bitcast.20, f32[2,256]{1,0:T(2,128)} %bitcast.21, bf16[2048,14336]{1,0:T(8,128)(2,1)} %bitcast.15, bf16[2048,14336]{1,0:T(8,128)(2,1)} %bitcast.16, bf16[14336,2048]{1,0:T(8,128)(2,1)} %bitcast.17), custom_call_target="tpu_custom_call" | custom-call | tf_op jit(solution)/shard_map/pallas_call | solution.py:241
  146.0 1.0 copy.9

commit v3 on v2

--- a/solution.py
+++ b/solution.py
@@ -16,7 +16,7 @@
 NT = 256
 PAIR = 2
 RING = 3
-EARLY = 8
+EARLY = 10
 LAG = 5
 COMM = True
 
@@ -96,7 +96,7 @@
 
     if COMM:
         pl.semaphore_wait(barrier, n - 1)
-        for mask in SENDS:
+        for mask in ORDER[1:NEAR]:
             send_z(mask).start()
     for q in range(1, RING):
         for c in fetch(q):
@@ -135,6 +135,10 @@
     def _(q):
         ready(q)
         up(q, 0, near // 2)
+
+    if COMM:
+        for mask in ORDER[NEAR:]:
+            send_z(mask).start()
 
     settle(4, NEAR)
 

time: 147 us -> 143 us (0.973)
  Pallas kernels: 146 us -> 142 us
    pallas_call x1, Pallas kernels: 146 us -> 142 us  [local(): pl.pallas_call(functools.partial(kernel, (n, slots, tokens, d, ff)), out_...]
where the time goes in v3:
time: 143 us
  Pallas kernels  142 us (99%)
    pallas_call x1, Pallas kernels, local(): pl.pallas_call(functools.partial(kernel, (n, slots, tokens, d, ff)), out_...  142 us

profile of v3, /device:TPU:0, one launch (start us, length us, event | category | flops | bytes accessed | tf_op | source)
XLA Modules:
  0.0 143.1 jit_solution(15797296915329650644)
XLA Ops:
  0.0 142.1 %shard_map.73 = bf16[256,2048]{1,0:T(8,128)(2,1)S(1)} custom-call(bf16[256,2048]{1,0:T(8,128)(2,1)} %bitcast.18, s32[2,256]{1,0:T(2,128)} %bitcast.19, s32[2,256]{1,0:T(2,128)} %bitcast.20, f32[2,256]{1,0:T(2,128)} %bitcast.21, bf16[2048,14336]{1,0:T(8,128)(2,1)} %bitcast.15, bf16[2048,14336]{1,0:T(8,128)(2,1)} %bitcast.16, bf16[14336,2048]{1,0:T(8,128)(2,1)} %bitcast.17), custom_call_target="tpu_custom_call" | custom-call | tf_op jit(solution)/shard_map/pallas_call | solution.py:245
  142.1 1.0 copy.9

commit v4 on v3

--- a/solution.py
+++ b/solution.py
@@ -17,7 +17,6 @@
 PAIR = 2
 RING = 3
 EARLY = 10
-LAG = 5
 COMM = True
 
 
@@ -189,14 +188,12 @@
             device_id=device(mask), device_id_type=MESH)
 
     def combine(t):
-        for u in (t, t + 1):
-            if COMM:
-                arrived = o_recv.at[u, pl.ds(1, n - 1)]
-                pltpu.make_async_copy(arrived, arrived, or_sem.at[u]).wait()
-        for u in (t, t + 1):
-            back = jnp.concatenate([o_recv[u, m].astype(f32) for m in range(n)], axis=0).astype(bf16)
-            y_ref[:, pl.ds(pl.multiple_of(u * NT, NT), NT)] = jnp.dot(
-                weight[...], back, preferred_element_type=f32).astype(bf16)
+        if COMM:
+            arrived = o_recv.at[t, pl.ds(1, n - 1)]
+            pltpu.make_async_copy(arrived, arrived, or_sem.at[t]).wait()
+        back = jnp.concatenate([o_recv[t, m].astype(f32) for m in range(n)], axis=0).astype(bf16)
+        y_ref[:, pl.ds(pl.multiple_of(t * NT, NT), NT)] = jnp.dot(
+            weight[...], back, preferred_element_type=f32).astype(bf16)
 
     @pl.loop(0, n_tiles)
     def _(t):
@@ -217,12 +214,10 @@
             for mask in FAR_FIRST:
                 send_o(t, mask).start()
 
-        @pl.when((t >= LAG) & (t % 2 == LAG % 2))
-        def _():
-            combine(t - LAG)
-
-    for t in range((n_tiles - LAG + 1) // 2 * 2, n_tiles, 2):
+    @pl.loop(0, n_tiles)
+    def _(t):
         combine(t)
+
     if COMM:
         for mask in SENDS:
             send_z(mask).wait_send()

time: 143 us -> 143 us (level)
  no operation moved by 1% of the time
where the time goes in v4:
time: 143 us
  Pallas kernels  142 us (99%)
    pallas_call x1, Pallas kernels, local(): pl.pallas_call(functools.partial(kernel, (n, slots, tokens, d, ff)), out_...  142 us

profile of v4, /device:TPU:0, one launch (start us, length us, event | category | flops | bytes accessed | tf_op | source)
XLA Modules:
  0.0 142.6 jit_solution(7133033869635927043)
XLA Ops:
  0.0 141.6 %shard_map.73 = bf16[256,2048]{1,0:T(8,128)(2,1)S(1)} custom-call(bf16[256,2048]{1,0:T(8,128)(2,1)} %bitcast.18, s32[2,256]{1,0:T(2,128)} %bitcast.19, s32[2,256]{1,0:T(2,128)} %bitcast.20, f32[2,256]{1,0:T(2,128)} %bitcast.21, bf16[2048,14336]{1,0:T(8,128)(2,1)} %bitcast.15, bf16[2048,14336]{1,0:T(8,128)(2,1)} %bitcast.16, bf16[14336,2048]{1,0:T(8,128)(2,1)} %bitcast.17), custom_call_target="tpu_custom_call" | custom-call | tf_op jit(solution)/shard_map/pallas_call | solution.py:240
  141.6 1.0 copy.9
